TPU v7x, 32 devices: a whole 2x2x4 slice. The times are simulated.
32 devices in a mesh: row: 4 (over z), col: 8 (over y, x, core).
Axes of the slice: x: 2, y: 2, z: 4, core: 2. Of those that a mesh axis runs over, the one named last changes fastest.
Arguments:
- residual: float32 [8192, 2048], P('row', 'col'), may hold values from -6 to 6
- point_spread: float32 [1024, 1024], P('col'), may hold values from -0.6 to 1
- peak_pixels: int32 [4, 64, 2], replicated, may hold values from 0 to 8191, as said below
Outputs:
- cleaned: float32 [8192, 2048], P('row', 'col')
- tile_peak: float32 [4, 8], P('row', 'col')
- components: float32 [4, 64], replicated
Inputs may be any that keep to these rules, and one draw needn't show every extreme that they name: peak_pixels[r, k, 0] is a row below 8192 and peak_pixels[r, k, 1] a column below 2048; positions may repeat.
All inputs are finite; a program needn't handle non-finite values.
Results may differ from a plain program's by a relative error of at most 0.00002.
Values sent between devices are 32-bit elements; how exact they have to be, the bound alone decides.
No kernel may reach another device: no remote copies, remote signals or barrier semaphores. Data moves between devices by JAX's collectives and lax.ppermute only.
A program may use at most 64 MiB of HBM per device.

v0:
```python
import jax
import jax.numpy as jnp
from jax import lax
from jax.sharding import PartitionSpec as P

loop_gain = 0.1


def subtract_rows(buffer, widened, row_offset, col_start, amplitudes, ordering, active):
    rows_here = widened.shape[0]
    tile_cols = buffer.shape[1]

    def remove_one(position, current):
        chosen = ordering[position]
        first_row = row_offset[chosen]
        window = lax.dynamic_slice(
            widened, (jnp.int32(0), col_start[chosen]), (rows_here, tile_cols)
        )
        before = lax.dynamic_slice(current, (first_row, jnp.int32(0)), (rows_here, tile_cols))
        return lax.dynamic_update_slice(
            current, before - amplitudes[chosen] * window, (first_row, jnp.int32(0))
        )

    return lax.fori_loop(0, active, remove_one, buffer)


def own_values(buffer, peak_rows, peak_cols, row_base, col_base, tile_rows, tile_cols, extent):
    local_rows = peak_rows - row_base
    local_cols = peak_cols - col_base
    owning = (
        (local_rows >= 0) & (local_rows < tile_rows) & (local_cols >= 0) & (local_cols < tile_cols)
    )
    picked = buffer[
        jnp.clip(local_rows, 0, tile_rows - 1) + extent, jnp.clip(local_cols, 0, tile_cols - 1)
    ]
    return jnp.where(owning, picked, 0.0)


def round_values(buffer, peak_rows, peak_cols, row_base, col_base, tile_rows, tile_cols, extent):
    partial_value = own_values(
        buffer, peak_rows, peak_cols, row_base, col_base, tile_rows, tile_cols, extent
    )
    return lax.psum(partial_value, ("row", "col"))


def local(residual, point_spread, peak_pixels):
    tile_rows, tile_cols = residual.shape
    extent = point_spread.shape[1]
    half_width = extent // 2
    rounds = peak_pixels.shape[0]
    row_base = lax.axis_index("row") * tile_rows
    col_base = lax.axis_index("col") * tile_cols
    buffer = jnp.pad(residual, ((extent, extent), (0, 0)))
    peak_rows = peak_pixels[:, :, 0]
    peak_cols = peak_pixels[:, :, 1]
    row_offset = peak_rows - row_base + half_width
    col_start = col_base - peak_cols + half_width + tile_cols
    inside = (
        (row_offset > 0)
        & (row_offset < tile_rows + extent)
        & (col_start > 0)
        & (col_start < extent + tile_cols)
    )
    ordering = jnp.argsort(jnp.where(inside, 0, 1).astype(jnp.int32), axis=1, stable=True)
    counts = jnp.sum(inside.astype(jnp.int32), axis=1)
    amplitudes = loop_gain * round_values(
        buffer, peak_rows[0], peak_cols[0], row_base, col_base, tile_rows, tile_cols, extent
    )
    assembled = lax.all_gather(point_spread, "col", axis=0, tiled=True)
    widened = jnp.pad(assembled, ((0, 0), (tile_cols, tile_cols)))
    buffer = subtract_rows(
        buffer, widened, row_offset[0], col_start[0], amplitudes, ordering[0], counts[0]
    )
    amplitude_rows = [amplitudes]
    for round_index in range(1, rounds):
        amplitudes = loop_gain * round_values(
            buffer,
            peak_rows[round_index],
            peak_cols[round_index],
            row_base,
            col_base,
            tile_rows,
            tile_cols,
            extent,
        )
        buffer = subtract_rows(
            buffer,
            widened,
            row_offset[round_index],
            col_start[round_index],
            amplitudes,
            ordering[round_index],
            counts[round_index],
        )
        amplitude_rows.append(amplitudes)
    cleaned = buffer[extent : extent + tile_rows]
    tile_peak = jnp.max(jnp.abs(cleaned)).reshape(1, 1)
    return (cleaned, tile_peak, jnp.stack(amplitude_rows))


def solution(mesh):
    return jax.shard_map(
        local,
        mesh=mesh,
        in_specs=(P("row", "col"), P("col", None), P()),
        out_specs=(P("row", "col"), P("row", "col"), P()),
        check_vma=False,
    )
```

profile of v0, /device:TPU:29, one launch (start us, length us, event | category | flops | bytes accessed | tf_op | source)
XLA Modules:
  0.0 1655.7 jit_solution(7925653327540661939)
XLA Ops:
  16.5 38.2 %psum.28 = f32[64]{0:T(128)S(1)} all-reduce(f32[64]{0:T(128)S(1)} %bitcast_select_fusion.3), channel_id=1, replica_groups=mesh['row'=4,'col'=8] {'row','col'}, use_global_device_ids=true, to_apply=%region_2.3 | all-reduce | flops 64 | bytes 512 | tf_op jit(solution)/shard_map/psum | solution.py:43
  55.8 5.7 pad.9
  61.5 130.2 %while.40 = (s32[]{:T(128)}, f32[4096,256]{1,0:T(8,128)}, s32[]{:T(128)}, s32[64]{0:T(128)S(1)}, s32[64]{0:T(128)S(1)}, /*index=5*/f32[64]{0:T(128)S(1)}, s32[64...) while((s32[]{:T(128)}, f32[4096,256]{1,0:T(8,128)}, ...), condition=%wide.region_4.5_spmd, body=%wide.region_3.4_spmd.sunk | while | flops 524302 | bytes 5243205 | solution.py:24
  73.5 4.1 dynamic_update_slice.16
  122.1 4.1 dynamic_update_slice.16
  154.5 4.1 dynamic_update_slice.16
  186.8 4.1 dynamic_update_slice.16
  194.6 312.5 %psum.29 = f32[64]{0:T(128)S(1)} all-reduce(f32[64]{0:T(128)S(1)} %bitcast_select_fusion.2), channel_id=1, replica_groups=mesh['row'=4,'col'=8] {'row','col'}, use_global_device_ids=true, to_apply=%region_5.6 | all-reduce | flops 64 | bytes 512 | tf_op jit(solution)/shard_map/psum | solution.py:43
  507.1 146.5 %while.41 = (s32[]{:T(128)}, f32[4096,256]{1,0:T(8,128)}, s32[]{:T(128)}, s32[64]{0:T(128)S(1)}, s32[64]{0:T(128)S(1)}, /*index=5*/f32[64]{0:T(128)S(1)}, s32[64...) while((s32[]{:T(128)}, f32[4096,256]{1,0:T(8,128)}, ...), condition=%wide.region_7.8_spmd, body=%wide.region_6.7_spmd.sunk | while | flops 524302 | bytes 5243205 | solution.py:24
  551.5 4.1 dynamic_update_slice.17
  616.4 4.1 dynamic_update_slice.17
  632.6 4.1 dynamic_update_slice.17
  656.3 280.8 %psum.30 = f32[64]{0:T(128)S(1)} all-reduce(f32[64]{0:T(128)S(1)} %bitcast_select_fusion.1), channel_id=1, replica_groups=mesh['row'=4,'col'=8] {'row','col'}, use_global_device_ids=true, to_apply=%region_8.9 | all-reduce | flops 64 | bytes 512 | tf_op jit(solution)/shard_map/psum | solution.py:43
  937.1 210.4 %while.42 = (s32[]{:T(128)}, f32[4096,256]{1,0:T(8,128)}, s32[]{:T(128)}, s32[64]{0:T(128)S(1)}, s32[64]{0:T(128)S(1)}, /*index=5*/f32[64]{0:T(128)S(1)}, s32[64...) while((s32[]{:T(128)}, f32[4096,256]{1,0:T(8,128)}, ...), condition=%wide.region_10.11_spmd, body=%wide.region_9.10_spmd.sunk | while | flops 524302 | bytes 5243205 | solution.py:24
  1013.7 4.1 dynamic_update_slice.18
  1094.4 4.1 dynamic_update_slice.18
  1126.7 4.1 dynamic_update_slice.18
  1150.0 117.7 %psum.31 = f32[64]{0:T(128)S(1)} all-reduce(f32[64]{0:T(128)S(1)} %bitcast_select_fusion), channel_id=1, replica_groups=mesh['row'=4,'col'=8] {'row','col'}, use_global_device_ids=true, to_apply=%region_11.12 | all-reduce | flops 64 | bytes 512 | tf_op jit(solution)/shard_map/psum | solution.py:43
  1267.7 376.8 %while.43 = (s32[]{:T(128)}, f32[4096,256]{1,0:T(8,128)}, s32[]{:T(128)}, s32[64]{0:T(128)S(1)}, s32[64]{0:T(128)S(1)}, /*index=5*/f32[64]{0:T(128)S(1)}, s32[64...) while((s32[]{:T(128)}, f32[4096,256]{1,0:T(8,128)}, ...), condition=%wide.region_13.14_spmd, body=%wide.region_12.13_spmd.sunk | while | flops 524302 | bytes 5243205 | solution.py:24
  1294.9 4.2 dynamic_update_slice.19
  1310.6 4.1 dynamic_update_slice.19
  1341.9 4.1 dynamic_update_slice.19
  1357.6 4.1 dynamic_update_slice.19
  1373.3 4.2 dynamic_update_slice.19
  1389.0 4.1 dynamic_update_slice.19
  1420.3 4.1 dynamic_update_slice.19
  1436.0 4.1 dynamic_update_slice.19
  1498.6 4.1 dynamic_update_slice.19
  1530.0 4.1 dynamic_update_slice.19
  1545.6 4.1 dynamic_update_slice.19
  1592.7 4.1 dynamic_update_slice.19
  1639.7 4.1 dynamic_update_slice.19
  (331 shorter events, 430.8 us)
Async XLA Ops:
  7.2 5.5 copy-start
  7.2 48.6 %all-gather.2.cloned.1.call-start = ((), (), s32[]{:S(2)}) async-start(), calls=%async_computation | async-start | bytes 4718592 | tf_op jit(solution)/shard_map/all_gather | solution.py:69
Sparse Core Ops, SparseCore 0:
  9.9 38.3 all-gather.1
where the time goes:
time: 1670 us; the launch traced here: 1660 us
  blocking collectives  749 us (45%)
  local copies, waits for them, and re-layouts  378 us (23%)
  loops' own time  361 us (22%)
  other arithmetic  152 us (9%)
    psum x4, blocking collectives, round_values(): return lax.psum(partial_value, ('row', 'col'))  749 us
    another operation x4, loops' own time, subtract_rows(): return lax.fori_loop(0, active, remove_one, buffer)  361 us
    dynamic_update_slice x54, local copies, waits for them, and re-layouts, remove_one(): lax.dynamic_update_slice(current, before - amplitudes[chosen] * window, (...  222 us
    sub x54, other arithmetic, remove_one(): before - amplitudes[chosen] * window  147 us
    dynamic_slice x54, local copies, waits for them, and re-layouts, remove_one(): col_start[chosen]  33.6 us
    dynamic_slice x54, local copies, waits for them, and re-layouts, remove_one(): amplitudes[chosen] * window  33.6 us
    dynamic_slice x54, local copies, waits for them, and re-layouts, remove_one(): chosen = ordering[position]  33.5 us
    dynamic_slice x54, local copies, waits for them, and re-layouts, remove_one(): first_row = row_offset[chosen]  33.5 us
  transfers between devices with their start and end apart: 1, of which 0 were waited for; matrix products, arithmetic and copies ran while one was open for 1% of the time, Pallas kernels for 0%

commit v1 on v0

--- a/solution.py
+++ b/solution.py
@@ -40,7 +40,7 @@
     partial_value = own_values(
         buffer, peak_rows, peak_cols, row_base, col_base, tile_rows, tile_cols, extent
     )
-    return lax.psum(partial_value, ("row", "col"))
+    return jnp.sum(lax.all_gather(partial_value, ("row", "col")), axis=0)
 
 
 def local(residual, point_spread, peak_pixels):

time: 1670 us -> 1630 us (0.976)
  blocking collectives: 749 us -> 712 us
    psum x4 -> x0, blocking collectives: 749 us -> none  [round_values(): return lax.psum(partial_value, ('row', 'col'))]
    all_gather x0 -> x4, blocking collectives: none -> 712 us  [round_values(): return jnp.sum(lax.all_gather(partial_value, ('row', 'col')), axis=0)]
where the time goes in v1:
time: 1630 us; the launch traced here: 1620 us
  blocking collectives  712 us (44%)
  local copies, waits for them, and re-layouts  378 us (23%)
  loops' own time  361 us (22%)
  other arithmetic  153 us (9%)
    all_gather x4, blocking collectives, round_values(): return jnp.sum(lax.all_gather(partial_value, ('row', 'col')), axis=0)  712 us
    another operation x4, loops' own time, subtract_rows(): return lax.fori_loop(0, active, remove_one, buffer)  361 us
    dynamic_update_slice x54, local copies, waits for them, and re-layouts, remove_one(): lax.dynamic_update_slice(current, before - amplitudes[chosen] * window, (...  222 us
    sub x54, other arithmetic, remove_one(): before - amplitudes[chosen] * window  147 us
    dynamic_slice x54, local copies, waits for them, and re-layouts, remove_one(): amplitudes[chosen] * window  33.6 us
    dynamic_slice x54, local copies, waits for them, and re-layouts, remove_one(): col_start[chosen]  33.6 us
    dynamic_slice x54, local copies, waits for them, and re-layouts, remove_one(): first_row = row_offset[chosen]  33.5 us
    dynamic_slice x54, local copies, waits for them, and re-layouts, remove_one(): chosen = ordering[position]  33.5 us
  transfers between devices with their start and end apart: 1, of which 0 were waited for; matrix products, arithmetic and copies ran while one was open for 1% of the time, Pallas kernels for 0%

profile of v1, /device:TPU:29, one launch (start us, length us, event | category | flops | bytes accessed | tf_op | source)
XLA Modules:
  0.0 1618.0 jit_solution(7974321947657330470)
XLA Ops:
  14.6 36.1 %all-gather = f32[32,1,64]{2,1,0:T(1,128)S(1)} all-gather(f32[1,1,64]{2,1,0:T(1,128)S(1)} %fusion.20), channel_id=1, replica_groups=mesh['row'=4,'col'=8] {'row','col'}, dimensions={0}, use_global_device_ids=true | all-gather | bytes 8448 | tf_op jit(solution)/shard_map/all_gather | solution.py:43
  53.0 5.7 pad.9
  58.7 130.2 %while.40 = (s32[]{:T(128)}, f32[4096,256]{1,0:T(8,128)}, s32[]{:T(128)}, s32[64]{0:T(128)S(1)}, s32[64]{0:T(128)S(1)}, /*index=5*/f32[64]{0:T(128)S(1)}, s32[64...) while((s32[]{:T(128)}, f32[4096,256]{1,0:T(8,128)}, ...), condition=%wide.region_4.5_spmd, body=%wide.region_3.4_spmd.sunk | while | flops 524302 | bytes 5243205 | solution.py:24
  70.8 4.1 dynamic_update_slice.16
  119.3 4.1 dynamic_update_slice.16
  151.7 4.1 dynamic_update_slice.16
  184.1 4.1 dynamic_update_slice.16
  191.8 295.1 %all-gather.1 = f32[32,1,64]{2,1,0:T(1,128)S(1)} all-gather(f32[1,1,64]{2,1,0:T(1,128)S(1)} %fusion.21), channel_id=1, replica_groups=mesh['row'=4,'col'=8] {'row','col'}, dimensions={0}, use_global_device_ids=true | all-gather | bytes 8448 | tf_op jit(solution)/shard_map/all_gather | solution.py:43
  487.0 146.5 %while.41 = (s32[]{:T(128)}, f32[4096,256]{1,0:T(8,128)}, s32[]{:T(128)}, s32[64]{0:T(128)S(1)}, s32[64]{0:T(128)S(1)}, /*index=5*/f32[64]{0:T(128)S(1)}, s32[64...) while((s32[]{:T(128)}, f32[4096,256]{1,0:T(8,128)}, ...), condition=%wide.region_7.8_spmd, body=%wide.region_6.7_spmd.sunk | while | flops 524302 | bytes 5243205 | solution.py:24
  531.5 4.1 dynamic_update_slice.17
  596.3 4.1 dynamic_update_slice.17
  612.5 4.1 dynamic_update_slice.17
  636.2 279.3 %all-gather.2 = f32[32,1,64]{2,1,0:T(1,128)S(1)} all-gather(f32[1,1,64]{2,1,0:T(1,128)S(1)} %fusion.22), channel_id=1, replica_groups=mesh['row'=4,'col'=8] {'row','col'}, dimensions={0}, use_global_device_ids=true | all-gather | bytes 8448 | tf_op jit(solution)/shard_map/all_gather | solution.py:43
  915.6 210.4 %while.42 = (s32[]{:T(128)}, f32[4096,256]{1,0:T(8,128)}, s32[]{:T(128)}, s32[64]{0:T(128)S(1)}, s32[64]{0:T(128)S(1)}, /*index=5*/f32[64]{0:T(128)S(1)}, s32[64...) while((s32[]{:T(128)}, f32[4096,256]{1,0:T(8,128)}, ...), condition=%wide.region_10.11_spmd, body=%wide.region_9.10_spmd.sunk | while | flops 524302 | bytes 5243205 | solution.py:24
  992.2 4.1 dynamic_update_slice.18
  1072.9 4.1 dynamic_update_slice.18
  1105.1 4.1 dynamic_update_slice.18
  1128.4 101.5 %all-gather.3 = f32[32,1,64]{2,1,0:T(1,128)S(1)} all-gather(f32[1,1,64]{2,1,0:T(1,128)S(1)} %fusion.23), channel_id=1, replica_groups=mesh['row'=4,'col'=8] {'row','col'}, dimensions={0}, use_global_device_ids=true | all-gather | bytes 8448 | tf_op jit(solution)/shard_map/all_gather | solution.py:43
  1230.0 376.9 %while.43 = (s32[]{:T(128)}, f32[4096,256]{1,0:T(8,128)}, s32[]{:T(128)}, s32[64]{0:T(128)S(1)}, s32[64]{0:T(128)S(1)}, /*index=5*/f32[64]{0:T(128)S(1)}, s32[64...) while((s32[]{:T(128)}, f32[4096,256]{1,0:T(8,128)}, ...), condition=%wide.region_13.14_spmd, body=%wide.region_12.13_spmd.sunk | while | flops 524302 | bytes 5243205 | solution.py:24
  1257.2 4.2 dynamic_update_slice.19
  1272.9 4.1 dynamic_update_slice.19
  1304.3 4.1 dynamic_update_slice.19
  1320.0 4.1 dynamic_update_slice.19
  1335.6 4.2 dynamic_update_slice.19
  1351.4 4.1 dynamic_update_slice.19
  1382.7 4.1 dynamic_update_slice.19
  1398.4 4.1 dynamic_update_slice.19
  1461.0 4.1 dynamic_update_slice.19
  1492.3 4.1 dynamic_update_slice.19
  1508.0 4.1 dynamic_update_slice.19
  1555.1 4.1 dynamic_update_slice.19
  1602.1 4.1 dynamic_update_slice.19
  (335 shorter events, 430.3 us)
Async XLA Ops:
  7.2 4.7 copy-start
  7.2 45.8 %all-gather.6.cloned.1.call-start = ((), (), s32[]{:S(2)}) async-start(), calls=%async_computation | async-start | bytes 4718592 | tf_op jit(solution)/shard_map/all_gather | solution.py:69
Sparse Core Ops, SparseCore 0:
  9.9 37.8 all-gather.5

commit v2 on v0

--- a/solution.py
+++ b/solution.py
@@ -40,7 +40,7 @@
     partial_value = own_values(
         buffer, peak_rows, peak_cols, row_base, col_base, tile_rows, tile_cols, extent
     )
-    return lax.psum(partial_value, ("row", "col"))
+    return lax.psum(lax.psum(partial_value, "row"), "col")
 
 
 def local(residual, point_spread, peak_pixels):

time: 1670 us -> 1610 us (0.964)
  blocking collectives: 749 us -> 673 us
    psum x4 -> x8, blocking collectives: 749 us -> 673 us  [round_values(): return lax.psum(lax.psum(partial_value, 'row'), 'col')]
  transfers between devices with their start and end apart: 1 -> 1, of which waited for: 0 -> 1; matrix products, arithmetic and copies ran while one was open for 1% -> 1% of each run, Pallas kernels for 0% -> 0%
where the time goes in v2:
time: 1610 us; the launch traced here: 1590 us
  blocking collectives  673 us (42%)
  local copies, waits for them, and re-layouts  378 us (23%)
  loops' own time  361 us (22%)
  other arithmetic  152 us (9%)
    psum x8, blocking collectives, round_values(): return lax.psum(lax.psum(partial_value, 'row'), 'col')  673 us
    another operation x4, loops' own time, subtract_rows(): return lax.fori_loop(0, active, remove_one, buffer)  361 us
    dynamic_update_slice x54, local copies, waits for them, and re-layouts, remove_one(): lax.dynamic_update_slice(current, before - amplitudes[chosen] * window, (...  222 us
    sub x54, other arithmetic, remove_one(): before - amplitudes[chosen] * window  147 us
    dynamic_slice x54, local copies, waits for them, and re-layouts, remove_one(): amplitudes[chosen] * window  33.6 us
    dynamic_slice x54, local copies, waits for them, and re-layouts, remove_one(): col_start[chosen]  33.6 us
    dynamic_slice x54, local copies, waits for them, and re-layouts, remove_one(): chosen = ordering[position]  33.5 us
    dynamic_slice x54, local copies, waits for them, and re-layouts, remove_one(): first_row = row_offset[chosen]  33.5 us
  transfers between devices with their start and end apart: 1, of which 1 were waited for; matrix products, arithmetic and copies ran while one was open for 1% of the time, Pallas kernels for 0%

profile of v2, /device:TPU:29, one launch (start us, length us, event | category | flops | bytes accessed | tf_op | source)
XLA Modules:
  0.0 1589.9 jit_solution(9138083974829281676)
XLA Ops:
  16.5 6.4 psum.56
  22.9 13.4 psum.57
  37.3 10.4 all-gather.2.cloned.1.call-done
  47.7 5.7 pad.9
  53.4 130.2 %while.40 = (s32[]{:T(128)}, f32[4096,256]{1,0:T(8,128)}, s32[]{:T(128)}, s32[64]{0:T(128)S(1)}, s32[64]{0:T(128)S(1)}, /*index=5*/f32[64]{0:T(128)S(1)}, s32[64...) while((s32[]{:T(128)}, f32[4096,256]{1,0:T(8,128)}, ...), condition=%wide.region_5.6_spmd, body=%wide.region_4.5_spmd.sunk | while | flops 524302 | bytes 5243205 | solution.py:24
  65.5 4.1 dynamic_update_slice.16
  178.8 4.1 dynamic_update_slice.16
  186.6 246.4 %psum.58 = f32[64]{0:T(128)S(1)} all-reduce(f32[64]{0:T(128)S(1)} %bitcast_select_fusion.2), channel_id=1, replica_groups=mesh['row'=4,'col'=8] {'row'}, use_global_device_ids=true, to_apply=%region_6.7 | all-reduce | flops 64 | bytes 512 | tf_op jit(solution)/shard_map/psum | solution.py:43
  433.0 46.0 %psum.59 = f32[64]{0:T(128)S(1)} all-reduce(f32[64]{0:T(128)S(1)} %psum.58), channel_id=1, replica_groups=mesh['row'=4,'col'=8] {'col'}, use_global_device_ids=true, to_apply=%region_7.8 | all-reduce | flops 64 | bytes 512 | tf_op jit(solution)/shard_map/psum | solution.py:43
  478.9 146.5 %while.41 = (s32[]{:T(128)}, f32[4096,256]{1,0:T(8,128)}, s32[]{:T(128)}, s32[64]{0:T(128)S(1)}, s32[64]{0:T(128)S(1)}, /*index=5*/f32[64]{0:T(128)S(1)}, s32[64...) while((s32[]{:T(128)}, f32[4096,256]{1,0:T(8,128)}, ...), condition=%wide.region_9.10_spmd, body=%wide.region_8.9_spmd.sunk | while | flops 524302 | bytes 5243205 | solution.py:24
  523.4 4.1 dynamic_update_slice.17
  588.3 4.1 dynamic_update_slice.17
  628.2 41.0 %psum.60 = f32[64]{0:T(128)S(1)} all-reduce(f32[64]{0:T(128)S(1)} %bitcast_select_fusion.1), channel_id=1, replica_groups=mesh['row'=4,'col'=8] {'row'}, use_global_device_ids=true, to_apply=%region_10.11 | all-reduce | flops 64 | bytes 512 | tf_op jit(solution)/shard_map/psum | solution.py:43
  669.2 221.1 %psum.61 = f32[64]{0:T(128)S(1)} all-reduce(f32[64]{0:T(128)S(1)} %psum.60), channel_id=1, replica_groups=mesh['row'=4,'col'=8] {'col'}, use_global_device_ids=true, to_apply=%region_11.12 | all-reduce | flops 64 | bytes 512 | tf_op jit(solution)/shard_map/psum | solution.py:43
  890.3 210.4 %while.42 = (s32[]{:T(128)}, f32[4096,256]{1,0:T(8,128)}, s32[]{:T(128)}, s32[64]{0:T(128)S(1)}, s32[64]{0:T(128)S(1)}, /*index=5*/f32[64]{0:T(128)S(1)}, s32[64...) while((s32[]{:T(128)}, f32[4096,256]{1,0:T(8,128)}, ...), condition=%wide.region_13.14_spmd, body=%wide.region_12.13_spmd.sunk | while | flops 524302 | bytes 5243205 | solution.py:24
  966.8 4.1 dynamic_update_slice.18
  1047.5 4.1 dynamic_update_slice.18
  1103.1 54.8 %psum.62 = f32[64]{0:T(128)S(1)} all-reduce(f32[64]{0:T(128)S(1)} %bitcast_select_fusion), channel_id=1, replica_groups=mesh['row'=4,'col'=8] {'row'}, use_global_device_ids=true, to_apply=%region_14.15 | all-reduce | flops 64 | bytes 512 | tf_op jit(solution)/shard_map/psum | solution.py:43
  1157.9 44.0 %psum.63 = f32[64]{0:T(128)S(1)} all-reduce(f32[64]{0:T(128)S(1)} %psum.62), channel_id=1, replica_groups=mesh['row'=4,'col'=8] {'col'}, use_global_device_ids=true, to_apply=%region_15.16 | all-reduce | flops 64 | bytes 512 | tf_op jit(solution)/shard_map/psum | solution.py:43
  1201.9 376.9 %while.43 = (s32[]{:T(128)}, f32[4096,256]{1,0:T(8,128)}, s32[]{:T(128)}, s32[64]{0:T(128)S(1)}, s32[64]{0:T(128)S(1)}, /*index=5*/f32[64]{0:T(128)S(1)}, s32[64...) while((s32[]{:T(128)}, f32[4096,256]{1,0:T(8,128)}, ...), condition=%wide.region_17.18_spmd, body=%wide.region_16.17_spmd.sunk | while | flops 524302 | bytes 5243205 | solution.py:24
  1229.1 4.2 dynamic_update_slice.19
  1244.8 4.1 dynamic_update_slice.19
  1276.1 4.1 dynamic_update_slice.19
  1291.8 4.1 dynamic_update_slice.19
  1307.5 4.2 dynamic_update_slice.19
  1323.2 4.1 dynamic_update_slice.19
  1354.6 4.1 dynamic_update_slice.19
  1370.2 4.1 dynamic_update_slice.19
  1432.9 4.1 dynamic_update_slice.19
  1464.2 4.1 dynamic_update_slice.19
  1479.9 4.1 dynamic_update_slice.19
  1527.0 4.1 dynamic_update_slice.19
  (335 shorter events, 451.4 us)
Async XLA Ops:
  7.2 5.5 copy-start
  7.2 40.6 %all-gather.2.cloned.1.call-start = ((), (), s32[]{:S(2)}) async-start(), calls=%async_computation | async-start | bytes 4718592 | tf_op jit(solution)/shard_map/all_gather | solution.py:69
Sparse Core Ops, SparseCore 0:
  9.9 37.8 all-gather.1
